TPU v7x, 32 devices: a whole 2x2x4 slice. The times are simulated.
32 devices in a mesh: head: 8 (over z, x), client: 4 (over y, core).
Axes of the slice: x: 2, y: 2, z: 4, core: 2. Of those that a mesh axis runs over, the one named last changes fastest.
Arguments:
- client_ids: int32 [32], replicated, may hold values from 0 to 127, as said below
- client_table: bfloat16 [128, 256], replicated, may hold values from -6 to 6
- in_weight: bfloat16 [256, 4096], P(None, 'client'), may hold values from -0.375 to 0.375
- in_bias: float32 [4096], P('client'), may hold values from -3 to 3
- head_weight: bfloat16 [4096, 131072], P('client', 'head'), may hold values from -0.09375 to 0.09375
- tokens: int32 [32, 256], P(('head', 'client')), may hold values from 0 to 255
- labels: int32 [32, 256], P(('head', 'client')), may hold values from 0 to 255
- byte_table: bfloat16 [256, 4096], P(None, 'client'), may hold values from -5.5 to 6.7
- out_table: bfloat16 [256, 4096], P(None, 'client'), may hold values from -5.625 to 5.625
Outputs:
- head_grad: bfloat16 [4096, 131072], P('client', 'head')
- in_grad: float32 [256, 4096], P(None, 'client')
- losses: float32 [32], P(('head', 'client'))
Inputs may be any that keep to these rules, and one draw needn't show every extreme that they name: `client_ids`: distinct population indices.
All inputs are finite; a program needn't handle non-finite values.
Results may differ from a plain program's by a relative error of at most 0.0085.
Values may be sent and summed in bfloat16 or wider, within the bound.
A program may use at most 128 MiB of HBM per device.

v0:
```python
import jax
import jax.numpy as jnp
from jax import lax
from jax.sharding import PartitionSpec as P

EPSILON = 1e-06
learn_rate = 0.1


def client_loss(factor_a, factor_b, inputs, label_row, out_table):
    depth = factor_a.shape[0]
    rank_size = factor_a.shape[1]
    normed_in = inputs * lax.rsqrt(jnp.mean(inputs * inputs, -1, keepdims=True) + EPSILON)
    low_rank = jnp.dot(normed_in, factor_a, precision=lax.Precision.HIGHEST)
    adapted = inputs + jnp.dot(low_rank, factor_b, precision=lax.Precision.HIGHEST) / jnp.sqrt(
        jnp.float32(depth * rank_size)
    )
    normed = (adapted * lax.rsqrt(jnp.mean(adapted * adapted, -1, keepdims=True) + EPSILON)).astype(
        jnp.bfloat16
    )
    logits = lax.dot_general(
        normed, out_table, (((1,), (1,)), ((), ())), preferred_element_type=jnp.float32
    )
    logits = logits * (4.0 / jnp.sqrt(jnp.float32(depth)))
    log_total = jax.nn.logsumexp(logits, -1)
    vocab_ids = lax.broadcasted_iota(jnp.int32, logits.shape, 1)
    picked = jnp.sum(jnp.where(vocab_ids == label_row[:, None], logits, 0.0), -1)
    return jnp.sum(log_total - picked)


def train_client(factor_row, token_row, label_row, byte_table, out_table):
    depth = byte_table.shape[1]
    split_at = factor_row.shape[0] // 2
    rank_size = split_at // depth
    start_a = factor_row[:split_at].reshape(depth, rank_size).astype(jnp.float32)
    start_b = factor_row[split_at:].reshape(rank_size, depth).astype(jnp.float32)
    onehot = (
        token_row[:, None]
        == lax.broadcasted_iota(jnp.int32, (token_row.shape[0], byte_table.shape[0]), 1)
    ).astype(jnp.bfloat16)
    inputs = jnp.dot(onehot, byte_table, preferred_element_type=jnp.float32)
    loss_grad = jax.value_and_grad(client_loss, argnums=(0, 1))
    first_loss, (grad_a, grad_b) = loss_grad(start_a, start_b, inputs, label_row, out_table)
    middle_a = start_a - learn_rate * grad_a
    middle_b = start_b - learn_rate * grad_b
    second_loss, (grad_a, grad_b) = loss_grad(middle_a, middle_b, inputs, label_row, out_table)
    final_a = middle_a - learn_rate * grad_a
    final_b = middle_b - learn_rate * grad_b
    deltas = jnp.concatenate(
        [(final_a - start_a).reshape(-1), (final_b - start_b).reshape(-1)]
    ).astype(jnp.bfloat16)
    return (deltas, first_loss / token_row.shape[0])


def local(
    client_ids, client_table, in_weight, in_bias, head_weight, tokens, labels, byte_table, out_table
):
    head_count = lax.axis_size("head")
    group_count = lax.axis_size("client")
    per_device = tokens.shape[0]
    byte_full, out_full = (
        lax.all_gather(byte_table, "client", axis=1, tiled=True),
        lax.all_gather(out_table, "client", axis=1, tiled=True),
    )
    ordered = client_ids.reshape(head_count, group_count, per_device).transpose(1, 0, 2).reshape(-1)
    chosen = client_table[ordered]
    preact = jnp.dot(chosen, in_weight, preferred_element_type=jnp.float32) + in_bias
    hidden = jnp.maximum(preact, 0.0).astype(jnp.bfloat16)
    hidden_rows = hidden
    summed = lax.psum_scatter(
        jnp.dot(hidden_rows, head_weight, preferred_element_type=jnp.float32),
        "client",
        scatter_dimension=0,
        tiled=True,
    )
    owned = lax.all_to_all(
        summed.astype(jnp.bfloat16), "head", split_axis=0, concat_axis=1, tiled=True
    )

    def run_client(record):
        return train_client(record[0], record[1], record[2], byte_full, out_full)

    deltas, losses = lax.map(run_client, (owned, tokens, labels))
    returned = lax.all_to_all(deltas, "head", split_axis=1, concat_axis=0, tiled=True)
    received = lax.all_gather(returned, "client", axis=0, tiled=True)
    hidden_rows = hidden
    grad_sum = lax.dot_general(
        hidden_rows, received, (((0,), (0,)), ((), ())), preferred_element_type=jnp.float32
    )
    partial_value = lax.dot_general(
        received, head_weight, (((1,), (1,)), ((), ())), preferred_element_type=jnp.float32
    )
    hidden_back = partial_value
    grad_sum, hidden_back = (grad_sum, hidden_back)
    hidden_back = lax.psum(hidden_back, "head")
    masked = jnp.where(preact > 0, hidden_back, 0.0)
    in_grad = lax.dot_general(
        chosen.astype(jnp.float32),
        masked,
        (((0,), (0,)), ((), ())),
        precision=lax.Precision.HIGHEST,
    )
    return (grad_sum.astype(jnp.bfloat16), in_grad, losses)


def solution(mesh):
    placed = (
        P(),
        P(),
        P(None, "client"),
        P("client"),
        P("client", "head"),
        P(("head", "client"), None),
        P(("head", "client"), None),
        P(None, "client"),
        P(None, "client"),
    )
    return jax.shard_map(
        local,
        mesh=mesh,
        in_specs=placed,
        out_specs=(P("client", "head"), P(None, "client"), P(("head", "client"))),
        check_vma=False,
    )
```

profile of v0, /device:TPU:0, one launch (start us, length us, event | category | flops | bytes accessed | tf_op | source)
XLA Modules:
  0.0 274.1 jit_solution(7337150185194927193)
XLA Ops:
  7.2 0.8 reshape.166
  8.2 1.5 gather_fusion
  9.7 0.9 convolution_add_fusion
  10.5 14.9 %fusion.59 = f32[32,16384]{1,0:T(8,128)} fusion(bf16[1024,16384]{1,0:T(8,128)(2,1)} %param.13, f32[32,1024]{1,0:T(8,128)S(1)} %convolution_add_fusion), kind=kOutput, calls=%fused_computation.91 | convolution fusion | flops 1073807360 | bytes 35782656 | tf_op jit(solution)/shard_map/dot_general | solution.py:71
  25.5 0.7 all-gather.5.cloned.1.call-update
  26.2 0.7 all-gather.7.cloned.1.call-update
  26.9 32.6 %reduce-scatter.2.cloned.1.call-done = f32[8,16384]{1,0:T(8,128)} async-done(((f32[32,16384]{1,0:T(8,128)}), f32[8,16384]{1,0:T(8,128)}) %reduce-scatter.2.cloned.1.call-update) | async-done | bytes 524304 | tf_op jit(solution)/shard_map/reduce_scatter | solution.py:70
  59.5 1.1 convert_bitcast_fusion
  60.6 0.5 broadcast.217
  61.1 0.8 reduce.4
  61.9 0.9 reshape.181
  62.8 5.5 %all-to-all-start = ((bf16[8,2,8192]{2,1,0:T(2,128)(2,1)}), bf16[8,2,8192]{2,1,0:T(2,128)(2,1)S(1)}, u32[]{:S(2)}, u32[]{:S(2)}) async-start(bf16[8,2,8192]{2,1,0:T(2,128)(2,1)} %reshape.181), calls=%async_computation.1 | async-start | bytes 524288 | tf_op jit(solution)/shard_map/all_to_all | solution.py:76
  68.3 15.3 %all-gather.5.cloned.1.call-done = bf16[256,4096]{1,0:T(8,128)(2,1)} async-done(((bf16[256,1024]{1,0:T(8,128)(2,1)}), bf16[256,4096]{1,0:T(8,128)(2,1)}) %all-gather.5.cloned.1.call-update) | async-done | bytes 2097168 | tf_op jit(solution)/shard_map/all_gather | solution.py:62
  83.7 4.4 %multiply_reduce_fusion.2 = (f32[256]{0:T(256)S(1)}, f32[256,4096]{1,0:T(8,128)}) fusion(bf16[256,4096]{1,0:T(8,128)(2,1)} %all-gather.5.cloned.1.call-done, s32[256]{0:T(256)S(1)} %bitcast.43), kind=kOutput, calls=%fused_computation.34 | convolution fusion | flops 539033344 | bytes 6293504 | tf_op jit(solution)/shard_map/while/body/eval_jaxpr/dot_general | solution.py:41
  88.0 0.8 reshape.182
  88.8 1.2 slice_reduce_fusion
  90.0 0.8 reshape.168
  90.9 0.3 copy.24
  91.2 5.0 %fusion.18 = f32[256,16]{0,1:T(8,128)S(1)} fusion(bf16[4096,16]{1,0:T(8,128)(2,1)S(1)} %reshape.168, f32[256,4096]{1,0:T(8,128)} %get-tuple-element.34, f32[256]{0:T(256)S(1)} %add_rsqrt_fusion), kind=kOutput, calls=%fused_computation.39 | convolution fusion | flops 202375168 | bytes 4342784 | tf_op jit(solution)/shard_map/while/body/eval_jaxpr/jvp()/dot_general | solution.py:14
  96.3 4.3 %multiply_reduce_fusion.1 = (f32[256]{0:T(256)S(1)}, f32[256,4096]{1,0:T(8,128)}) fusion(f32[256,4096]{1,0:T(8,128)S(1)} %copy-done.2, f32[256,16]{0,1:T(8,128)S(1)} %fusion.18, bf16[16,4096]{1,0:T(8,128)(2,1)S(1)} %reshape.169), kind=kOutput, calls=%fused_computation.33 | convolution fusion | flops 205520640 | bytes 8537088 | tf_op jit(solution)/shard_map/while/body/eval_jaxpr/jvp()/dot_general | solution.py:15
  100.6 7.2 %all-gather.7.cloned.1.call-done = bf16[256,4096]{1,0:T(8,128)(2,1)} async-done(((bf16[256,1024]{1,0:T(8,128)(2,1)}), bf16[256,4096]{1,0:T(8,128)(2,1)}) %all-gather.7.cloned.1.call-update) | async-done | bytes 2097168 | tf_op jit(solution)/shard_map/all_gather | solution.py:63
  107.8 3.9 %fusion.78 = (f32[256]{0:T(256)S(1)}, f32[256,256]{0,1:T(8,128)S(1)}) fusion(bf16[256,4096]{1,0:T(8,128)(2,1)} %all-gather.7.cloned.1.call-done, f32[256,4096]{1,0:T(8,128)} %get-tuple-element.36, f32[256]{0:T(256)S(1)} %fusion.60), kind=kOutput, calls=%fused_computation.118 | convolution fusion | flops 539098880 | bytes 6555648 | tf_op jit(solution)/shard_map/while/body/eval_jaxpr/jvp()/dot_general | solution.py:21
  111.8 0.6 subtract_reduce_fusion
  112.5 0.9 fusion.10
  113.5 2.8 %fusion.76 = f32[256,16]{0,1:T(8,128)S(1)} fusion(bf16[16,4096]{1,0:T(8,128)(2,1)S(1)} %reshape.169, bf16[256,4096]{1,0:T(8,128)(2,1)S(1)} %get-tuple-element.40, f32[256,4096]{1,0:T(8,128)S(1)} %copy-done.4, f32[256]{0:T(256)S(1)} %multiply_multiply_fusion.1, f32[256]{0:T(256)S(1)} %fusion.60), kind=kOutput, calls=%fused_computation.117 | convolution fusion | flops 207618048 | bytes 6440960 | tf_op jit(solution)/shard_map/while/body/eval_jaxpr/transpose(jvp())/dot_general | solution.py:15
  116.3 3.1 %fusion.6 = f32[16,4096]{1,0:T(8,128)S(1)} fusion(f32[256,16]{0,1:T(8,128)S(1)} %fusion.18, bf16[16,4096]{1,0:T(8,128)(2,1)S(1)} %reshape.169, bf16[256,4096]{1,0:T(8,128)(2,1)S(1)} %get-tuple-element.40, f32[256,4096]{1,0:T(8,128)S(1)} %copy-done.4, f32[256]{0:T(256)S(1)} %multiply_multiply_fusion.1, f32[256]{0:T(256)S(1)} %fusion.60), kind=kOutput, calls=%fused_computation.21 | convolution fusion | flops 207814656 | bytes 6703104 | tf_op jit(solution)/shard_map/while/body/eval_jaxpr/transpose(jvp())/dot_general | solution.py:15
  119.4 2.5 fusion.7
  121.9 3.4 %fusion.15 = f32[256,16]{0,1:T(8,128)S(1)} fusion(f32[4096,16]{0,1:T(8,128)S(1)} %fusion.7, f32[256,4096]{1,0:T(8,128)S(1)} %copy-done.3, f32[256]{0:T(256)S(1)} %add_rsqrt_fusion), kind=kOutput, calls=%fused_computation.36 | convolution fusion | flops 202375168 | bytes 4473856 | tf_op jit(solution)/shard_map/while/body/eval_jaxpr/jvp()/dot_general | solution.py:14
  125.4 4.1 %multiply_reduce_fusion = (f32[256]{0:T(256)S(1)}, f32[256,4096]{1,0:T(8,128)S(1)}) fusion(f32[256,4096]{1,0:T(8,128)S(1)} %copy-done.3, f32[256,16]{0,1:T(8,128)S(1)} %fusion.15, f32[16,4096]{1,0:T(8,128)S(1)} %fusion.6), kind=kOutput, calls=%fused_computation.31 | convolution fusion | flops 205520640 | bytes 8668160 | tf_op jit(solution)/shard_map/while/body/eval_jaxpr/jvp()/dot_general | solution.py:15
  129.5 0.9 fusion.79
  130.4 0.9 fusion.11
  131.4 4.2 %fusion.73 = f32[256,16]{0,1:T(8,128)S(1)} fusion(f32[16,4096]{1,0:T(8,128)S(1)} %fusion.6, bf16[256,4096]{1,0:T(8,128)(2,1)S(1)} %get-tuple-element.46, f32[256,4096]{1,0:T(8,128)S(1)} %get-tuple-element.42, f32[256]{0:T(256)S(1)} %multiply_multiply_fusion, f32[256]{0:T(256)S(1)} %fusion.61), kind=kOutput, calls=%fused_computation.116 | convolution fusion | flops 207618048 | bytes 6572032 | tf_op jit(solution)/shard_map/while/body/eval_jaxpr/transpose(jvp())/dot_general | solution.py:15
  135.6 2.9 %fusion.9 = bf16[16,4096]{1,0:T(8,128)(2,1)S(1)} fusion(f32[16,4096]{1,0:T(8,128)S(1)} %fusion.6, f32[256,16]{0,1:T(8,128)S(1)} %fusion.15, bf16[16,4096]{1,0:T(8,128)(2,1)S(1)} %reshape.169, bf16[256,4096]{1,0:T(8,128)(2,1)S(1)} %get-tuple-element.46, f32[256,4096]{1,0:T(8,128)S(1)} %get-tuple-element.42, f32[256]{0:T(256)S(1)} %multiply_multiply_fusion, ...), kind=kOutput, calls=%fused_computation.25 | convolution fusion | flops 207945728 | bytes 6834176 | tf_op jit(solution)/shard_map/while/body/eval_jaxpr/transpose(jvp())/dot_general | solution.py:15
  138.5 2.5 fusion.8
  141.0 0.5 copy.25
  141.5 1.2 concatenate.17
  142.7 0.2 concatenate.18
  143.0 0.4 copy.29
  143.4 2.2 reduce.5
  145.7 0.2 reshape.183
  145.8 14.9 %all_to_all.26 = bf16[8,2,8192]{2,1,0:T(2,128)(2,1)S(1)} all-to-all(bf16[8,2,8192]{2,1,0:T(2,128)(2,1)S(1)} %reshape.183), channel_id=1, replica_groups=mesh['head'=8,'client'=4] {'head'}, dimensions={0} | all-to-all | bytes 524288 | tf_op jit(solution)/shard_map/all_to_all | solution.py:84
  160.7 0.3 reshape.184
  161.0 1.0 copy.27
  162.6 14.3 %all-gather.9.cloned.1.call-done = bf16[1,32,16384]{2,1,0:T(8,128)(2,1)} async-done(((bf16[1,8,16384]{2,1,0:T(8,128)(2,1)}), bf16[1,32,16384]{2,1,0:T(8,128)(2,1)}) %all-gather.9.cloned.1.call-update) | async-done | bytes 1048592 | tf_op jit(solution)/shard_map/all_gather | solution.py:85
  177.0 16.1 %fusion.30 = f32[32,1024]{1,0:T(8,128)} fusion(bf16[1024,16384]{1,0:T(8,128)(2,1)} %param.13, bf16[1,32,16384]{2,1,0:T(8,128)(2,1)} %all-gather.9.cloned.1.call-done), kind=kOutput, calls=%fused_computation.52 | convolution fusion | flops 1073741824 | bytes 34734080 | tf_op jit(solution)/shard_map/dot_general | solution.py:90
  193.1 14.9 %convolution_convert_fusion = bf16[1024,16384]{1,0:T(8,128)(2,1)} fusion(bf16[1,32,16384]{2,1,0:T(8,128)(2,1)S(1)} %copy-done.6, f32[32,1024]{1,0:T(8,128)S(1)} %convolution_add_fusion), kind=kOutput, calls=%fused_computation.1 | convolution fusion | flops 1090584576 | bytes 34734080 | tf_op jit(solution)/shard_map/dot_general | solution.py:87
  207.9 55.7 %all-reduce.2.cloned.1.call-done = f32[32,1024]{1,0:T(8,128)} async-done(((f32[32,1024]{1,0:T(8,128)}), f32[32,1024]{1,0:T(8,128)}) %all-reduce.2.cloned.1.call-update) | async-done | bytes 131088 | tf_op jit(solution)/shard_map/psum | solution.py:95
  263.7 2.5 fusion.42
  (43 shorter events, 1.1 us)
Async XLA Ops:
  7.2 2.5 copy-start
  7.2 52.3 %reduce-scatter.2.cloned.1.call-start = ((), (), s32[]{:S(2)}) async-start(), calls=%async_computation.3 | async-start | bytes 2621440 | tf_op jit(solution)/shard_map/reduce_scatter | solution.py:70
  25.4 58.2 %copy-start.7 = (s32[1,256]{1,0:T(1,128)S(1)}, s32[1,256]{1,0:T(1,128)}, u32[]{:S(2)}) copy-start(s32[1,256]{1,0:T(1,128)} %param.14) | copy-start | bytes 3076
  25.4 58.2 %all-gather.5.cloned.1.call-start = ((), (), s32[]{:S(2)}) async-start(), calls=%async_computation.4 | async-start | bytes 2621440 | tf_op jit(solution)/shard_map/all_gather | solution.py:62
  26.2 81.6 %all-gather.7.cloned.1.call-start = ((), (), s32[]{:S(2)}) async-start(), calls=%async_computation.5 | async-start | bytes 2621440 | tf_op jit(solution)/shard_map/all_gather | solution.py:63
  62.8 25.2 %all-to-all-start = ((bf16[8,2,8192]{2,1,0:T(2,128)(2,1)}), bf16[8,2,8192]{2,1,0:T(2,128)(2,1)S(1)}, u32[]{:S(2)}, u32[]{:S(2)}) async-start(bf16[8,2,8192]{2,1,0:T(2,128)(2,1)} %reshape.181), calls=%async_computation.1 | async-start | bytes 524288 | tf_op jit(solution)/shard_map/all_to_all | solution.py:76
  68.3 108.7 %all-gather.9.cloned.1.call-start = ((), (), s32[]{:S(2)}) async-start(), calls=%async_computation.7 | async-start | bytes 1310720 | tf_op jit(solution)/shard_map/all_gather | solution.py:85
  91.2 5.1 %copy-start.2 = (f32[256,4096]{1,0:T(8,128)S(1)}, f32[256,4096]{1,0:T(8,128)}, u32[]{:S(2)}) copy-start(f32[256,4096]{1,0:T(8,128)} %get-tuple-element.34) | copy-start | bytes 12582916
  100.6 11.1 %copy-start.8 = (s32[1,256]{1,0:T(1,128)S(1)}, s32[1,256]{1,0:T(1,128)}, u32[]{:S(2)}) copy-start(s32[1,256]{1,0:T(1,128)} %param.15) | copy-start | bytes 3076
  107.8 4.6 %copy-start.4 = (f32[256,4096]{1,0:T(8,128)S(1)}, f32[256,4096]{1,0:T(8,128)}, u32[]{:S(2)}) copy-start(f32[256,4096]{1,0:T(8,128)} %get-tuple-element.36) | copy-start | bytes 12582916
  107.8 4.7 %copy-start.5 = (bf16[256,4096]{1,0:T(8,128)(2,1)S(1)}, bf16[256,4096]{1,0:T(8,128)(2,1)}, u32[]{:S(2)}) copy-start(bf16[256,4096]{1,0:T(8,128)(2,1)} %all-gather.7.cloned.1.call-done) | copy-start | bytes 6291460
  116.3 3.1 %copy-start.3 = (f32[256,4096]{1,0:T(8,128)S(1)}, f32[256,4096]{1,0:T(8,128)}, u32[]{:S(2)}) copy-start(f32[256,4096]{1,0:T(8,128)} %get-tuple-element.34) | copy-start | bytes 12582916
  162.0 101.7 %all-reduce.2.cloned.1.call-start = ((), (), s32[]{:S(2)}) async-start(), calls=%async_computation.6 | async-start | bytes 262144 | tf_op jit(solution)/shard_map/psum | solution.py:95
  177.0 16.1 %copy-start.6 = (bf16[1,32,16384]{2,1,0:T(8,128)(2,1)S(1)}, bf16[1,32,16384]{2,1,0:T(8,128)(2,1)}, u32[]{:S(2)}) copy-start(bf16[1,32,16384]{2,1,0:T(8,128)(2,1)} %all-gather.9.cloned.1.call-done) | copy-start | bytes 3145732
  193.1 73.1 %copy-start.1 = (bf16[256,1024]{1,0:T(8,128)(2,1)S(1)}, bf16[256,1024]{1,0:T(8,128)(2,1)}, u32[]{:S(2)}) copy-start(bf16[256,1024]{1,0:T(8,128)(2,1)} %param.11) | copy-start | bytes 1572868
Sparse Core Ops, SparseCore 0:
  25.6 33.9 reduce-scatter.1
  61.1 22.5 all-gather.4
  85.2 22.5 all-gather.6
  162.1 14.7 all-gather.8
  193.2 70.4 all-reduce.1
where the time goes:
time: 278 us; the launch traced here: 274 us
  waiting for transfers between devices  127 us (46%)
  matrix products  95 us (34%)
  between operations  15.9 us (6%)
  blocking collectives  14.9 us (5%)
  local copies, waits for them, and re-layouts  10.8 us (4%)
  starting transfers between devices  5.69 us (2%)
  other arithmetic  5.08 us (2%)
    psum x1, waiting for transfers between devices, local(): hidden_back = lax.psum(hidden_back, 'head')  55.7 us
    reduce_scatter x1, waiting for transfers between devices, local(): lax.psum_scatter(jnp.dot(hidden_rows, head_weight, preferred_element_type...  32.6 us
    dot_general x6, matrix products, client_loss(): jnp.dot(low_rank, factor_b, precision=lax.Precision.HIGHEST)  21.5 us
    dot_general x1, matrix products, local(): lax.dot_general(received, head_weight, (((1,), (1,)), ((), ())), preferre...  16.1 us
    all_gather x1, waiting for transfers between devices, local(): lax.all_gather(byte_table, 'client', axis=1, tiled=True)  15.3 us
    all_to_all x1, blocking collectives, local(): lax.all_to_all(deltas, 'head', split_axis=1, concat_axis=0, tiled=True)  14.9 us
    dot_general x1, matrix products, local(): lax.dot_general(hidden_rows, received, (((0,), (0,)), ((), ())), preferre...  14.9 us
    dot_general x1, matrix products, local(): jnp.dot(hidden_rows, head_weight, preferred_element_type=jnp.float32)  14.9 us
  transfers between devices with their start and end apart: 6, of which 5 were waited for; matrix products, arithmetic and copies ran while one was open for 13% of the time, Pallas kernels for 0%

commit v1 on v0

--- a/solution.py
+++ b/solution.py
@@ -5,6 +5,22 @@
 
 EPSILON = 1e-06
 learn_rate = 0.1
+
+
+def swapped_with_each(shard, axis, split, join):
+    ways, here = (lax.axis_size(axis), lax.axis_index(axis))
+    width = shard.shape[split] // ways
+    shape = list(shard.shape)
+    shape[split] = width
+    height = shape[join]
+    shape[join] = height * ways
+    full = jnp.zeros(shape, shard.dtype)
+    for mask in range(ways):
+        part = lax.dynamic_slice_in_dim(shard, (here ^ mask) * width, width, axis=split)
+        if mask:
+            part = lax.ppermute(part, axis, [(d, d ^ mask) for d in range(ways)])
+        full = lax.dynamic_update_slice_in_dim(full, part, (here ^ mask) * height, axis=join)
+    return full
 
 
 def client_loss(factor_a, factor_b, inputs, label_row, out_table):
@@ -81,7 +97,7 @@
         return train_client(record[0], record[1], record[2], byte_full, out_full)
 
     deltas, losses = lax.map(run_client, (owned, tokens, labels))
-    returned = lax.all_to_all(deltas, "head", split_axis=1, concat_axis=0, tiled=True)
+    returned = swapped_with_each(deltas, "head", 1, 0)
     received = lax.all_gather(returned, "client", axis=0, tiled=True)
     hidden_rows = hidden
     grad_sum = lax.dot_general(

time: 278 us -> 282 us (1.014)
  blocking collectives: 14.9 us -> 0 us
  starting transfers between devices: 5.69 us -> 17.2 us
  local copies, waits for them, and re-layouts: 10.8 us -> 18.8 us
    all_to_all x1 -> x0, blocking collectives: 14.9 us -> none  [local(): lax.all_to_all(deltas, 'head', split_axis=1, concat_axis=0, tiled=True)]
    ppermute x0 -> x7, starting transfers between devices: none -> 11.5 us  [swapped_with_each(): part = lax.ppermute(part, axis, [(d, d ^ mask) for d in range(ways)])]
    dynamic_update_slice x0 -> x8, local copies, waits for them, and re-layouts: none -> 9.35 us  [swapped_with_each(): lax.dynamic_update_slice_in_dim(full, part, (here ^ mask) * height, axis=...]
  transfers between devices with their start and end apart: 6 -> 13, of which waited for: 5 -> 5; matrix products, arithmetic and copies ran while one was open for 13% -> 16% of each run, Pallas kernels for 0% -> 0%
where the time goes in v1:
time: 282 us; the launch traced here: 278 us
  waiting for transfers between devices  128 us (45%)
  matrix products  95 us (34%)
  local copies, waits for them, and re-layouts  18.8 us (7%)
  starting transfers between devices  17.2 us (6%)
  between operations  16.2 us (6%)
    psum x1, waiting for transfers between devices, local(): hidden_back = lax.psum(hidden_back, 'head')  55.7 us
    reduce_scatter x1, waiting for transfers between devices, local(): lax.psum_scatter(jnp.dot(hidden_rows, head_weight, preferred_element_type...  32.5 us
    dot_general x6, matrix products, client_loss(): jnp.dot(low_rank, factor_b, precision=lax.Precision.HIGHEST)  21.5 us
    all_gather x1, waiting for transfers between devices, local(): received = lax.all_gather(returned, 'client', axis=0, tiled=True)  16.2 us
    dot_general x1, matrix products, local(): lax.dot_general(received, head_weight, (((1,), (1,)), ((), ())), preferre...  16.1 us
    all_gather x1, waiting for transfers between devices, local(): lax.all_gather(byte_table, 'client', axis=1, tiled=True)  15.3 us
    dot_general x1, matrix products, local(): lax.dot_general(hidden_rows, received, (((0,), (0,)), ((), ())), preferre...  14.9 us
    dot_general x1, matrix products, local(): jnp.dot(hidden_rows, head_weight, preferred_element_type=jnp.float32)  14.9 us
  transfers between devices with their start and end apart: 13, of which 5 were waited for; matrix products, arithmetic and copies ran while one was open for 16% of the time, Pallas kernels for 0%

profile of v1, /device:TPU:0, one launch (start us, length us, event | category | flops | bytes accessed | tf_op | source)
XLA Modules:
  0.0 278.4 jit_solution(8159362830154557964)
XLA Ops:
  7.2 0.8 reshape.137
  8.2 1.5 gather_fusion
  9.7 0.9 convolution_add_fusion
  10.5 14.9 %fusion.57 = f32[32,16384]{1,0:T(8,128)} fusion(bf16[1024,16384]{1,0:T(8,128)(2,1)} %param.13, f32[32,1024]{1,0:T(8,128)S(1)} %convolution_add_fusion), kind=kOutput, calls=%fused_computation.88 | convolution fusion | flops 1073807360 | bytes 35782656 | tf_op jit(solution)/shard_map/dot_general | solution.py:87
  25.5 0.7 all-gather.4.cloned.1.call-update
  27.0 32.5 %reduce-scatter.2.cloned.1.call-done = f32[8,16384]{1,0:T(8,128)} async-done(((f32[32,16384]{1,0:T(8,128)}), f32[8,16384]{1,0:T(8,128)}) %reduce-scatter.2.cloned.1.call-update) | async-done | bytes 524304 | tf_op jit(solution)/shard_map/reduce_scatter | solution.py:86
  59.5 1.1 convert_bitcast_fusion
  61.1 0.8 reduce.4
  61.9 0.9 reshape.153
  62.8 5.5 %all-to-all-start = ((bf16[8,2,8192]{2,1,0:T(2,128)(2,1)}), bf16[8,2,8192]{2,1,0:T(2,128)(2,1)S(1)}, u32[]{:S(2)}, u32[]{:S(2)}) async-start(bf16[8,2,8192]{2,1,0:T(2,128)(2,1)} %reshape.153), calls=%async_computation.1 | async-start | bytes 524288 | tf_op jit(solution)/shard_map/all_to_all | solution.py:92
  68.3 15.3 %all-gather.4.cloned.1.call-done = bf16[256,4096]{1,0:T(8,128)(2,1)} async-done(((bf16[256,1024]{1,0:T(8,128)(2,1)}), bf16[256,4096]{1,0:T(8,128)(2,1)}) %all-gather.4.cloned.1.call-update) | async-done | bytes 2097168 | tf_op jit(solution)/shard_map/all_gather | solution.py:78
  83.7 4.4 %multiply_reduce_fusion.2 = (f32[256]{0:T(256)S(1)}, f32[256,4096]{1,0:T(8,128)}) fusion(bf16[256,4096]{1,0:T(8,128)(2,1)} %all-gather.4.cloned.1.call-done, s32[256]{0:T(256)S(1)} %bitcast.38), kind=kOutput, calls=%fused_computation.34 | convolution fusion | flops 539033344 | bytes 6293504 | tf_op jit(solution)/shard_map/while/body/eval_jaxpr/dot_general | solution.py:57
  88.0 0.8 reshape.154
  88.8 1.2 slice_reduce_fusion.1
  90.0 0.8 reshape.139
  91.2 5.0 %fusion.18 = f32[256,16]{0,1:T(8,128)S(1)} fusion(bf16[4096,16]{1,0:T(8,128)(2,1)S(1)} %reshape.139, f32[256,4096]{1,0:T(8,128)} %get-tuple-element.42, f32[256]{0:T(256)S(1)} %add_rsqrt_fusion), kind=kOutput, calls=%fused_computation.39 | convolution fusion | flops 202375168 | bytes 4342784 | tf_op jit(solution)/shard_map/while/body/eval_jaxpr/jvp()/dot_general | solution.py:30
  96.3 4.3 %multiply_reduce_fusion.1 = (f32[256]{0:T(256)S(1)}, f32[256,4096]{1,0:T(8,128)}) fusion(f32[256,4096]{1,0:T(8,128)S(1)} %copy-done.2, f32[256,16]{0,1:T(8,128)S(1)} %fusion.18, bf16[16,4096]{1,0:T(8,128)(2,1)S(1)} %reshape.140), kind=kOutput, calls=%fused_computation.33 | convolution fusion | flops 205520640 | bytes 8537088 | tf_op jit(solution)/shard_map/while/body/eval_jaxpr/jvp()/dot_general | solution.py:31
  100.6 7.2 %all-gather.6.cloned.1.call-done = bf16[256,4096]{1,0:T(8,128)(2,1)} async-done(((bf16[256,1024]{1,0:T(8,128)(2,1)}), bf16[256,4096]{1,0:T(8,128)(2,1)}) %all-gather.6.cloned.1.call-update) | async-done | bytes 2097168 | tf_op jit(solution)/shard_map/all_gather | solution.py:79
  107.8 3.9 %fusion.77 = (f32[256]{0:T(256)S(1)}, f32[256,256]{0,1:T(8,128)S(1)}) fusion(bf16[256,4096]{1,0:T(8,128)(2,1)} %all-gather.6.cloned.1.call-done, f32[256,4096]{1,0:T(8,128)} %get-tuple-element.44, f32[256]{0:T(256)S(1)} %fusion.58), kind=kOutput, calls=%fused_computation.118 | convolution fusion | flops 539098880 | bytes 6555648 | tf_op jit(solution)/shard_map/while/body/eval_jaxpr/jvp()/dot_general | solution.py:37
  112.5 0.9 fusion.10
  113.5 2.8 %fusion.74 = f32[256,16]{0,1:T(8,128)S(1)} fusion(bf16[16,4096]{1,0:T(8,128)(2,1)S(1)} %reshape.140, bf16[256,4096]{1,0:T(8,128)(2,1)S(1)} %get-tuple-element.48, f32[256,4096]{1,0:T(8,128)S(1)} %copy-done.4, f32[256]{0:T(256)S(1)} %multiply_multiply_fusion.1, f32[256]{0:T(256)S(1)} %fusion.58), kind=kOutput, calls=%fused_computation.116 | convolution fusion | flops 207618048 | bytes 6440960 | tf_op jit(solution)/shard_map/while/body/eval_jaxpr/transpose(jvp())/dot_general | solution.py:31
  116.3 3.1 %fusion.6 = f32[16,4096]{1,0:T(8,128)S(1)} fusion(f32[256,16]{0,1:T(8,128)S(1)} %fusion.18, bf16[16,4096]{1,0:T(8,128)(2,1)S(1)} %reshape.140, bf16[256,4096]{1,0:T(8,128)(2,1)S(1)} %get-tuple-element.48, f32[256,4096]{1,0:T(8,128)S(1)} %copy-done.4, f32[256]{0:T(256)S(1)} %multiply_multiply_fusion.1, f32[256]{0:T(256)S(1)} %fusion.58), kind=kOutput, calls=%fused_computation.21 | convolution fusion | flops 207814656 | bytes 6703104 | tf_op jit(solution)/shard_map/while/body/eval_jaxpr/transpose(jvp())/dot_general | solution.py:31
  119.4 2.5 fusion.7
  122.0 3.4 %fusion.15 = f32[256,16]{0,1:T(8,128)S(1)} fusion(f32[4096,16]{0,1:T(8,128)S(1)} %fusion.7, f32[256,4096]{1,0:T(8,128)S(1)} %copy-done.3, f32[256]{0:T(256)S(1)} %add_rsqrt_fusion), kind=kOutput, calls=%fused_computation.36 | convolution fusion | flops 202375168 | bytes 4473856 | tf_op jit(solution)/shard_map/while/body/eval_jaxpr/jvp()/dot_general | solution.py:30
  125.4 4.1 %multiply_reduce_fusion = (f32[256]{0:T(256)S(1)}, f32[256,4096]{1,0:T(8,128)S(1)}) fusion(f32[256,4096]{1,0:T(8,128)S(1)} %copy-done.3, f32[256,16]{0,1:T(8,128)S(1)} %fusion.15, f32[16,4096]{1,0:T(8,128)S(1)} %fusion.6), kind=kOutput, calls=%fused_computation.31 | convolution fusion | flops 205520640 | bytes 8668160 | tf_op jit(solution)/shard_map/while/body/eval_jaxpr/jvp()/dot_general | solution.py:31
  129.5 0.9 fusion.78
  130.4 0.9 fusion.11
  131.4 3.2 %fusion.30 = bf16[2,32,8,128]{3,2,1,0:T(8,128)(2,1)S(1)} fusion(f32[16,4096]{1,0:T(8,128)S(1)} %fusion.6, f32[256,16]{0,1:T(8,128)S(1)} %fusion.15, bf16[16,4096]{1,0:T(8,128)(2,1)S(1)} %reshape.140, bf16[256,4096]{1,0:T(8,128)(2,1)S(1)} %get-tuple-element.54, f32[256,4096]{1,0:T(8,128)S(1)} %get-tuple-element.50, f32[256]{0:T(256)S(1)} %multiply_multiply_fusion, ...), kind=kOutput, calls=%fused_computation.51 | convolution fusion | flops 207945728 | bytes 6834176 | tf_op jit(solution)/shard_map/while/body/eval_jaxpr/transpose(jvp())/dot_general | solution.py:31
  134.5 4.0 %fusion.71 = f32[256,16]{0,1:T(8,128)S(1)} fusion(f32[16,4096]{1,0:T(8,128)S(1)} %fusion.6, bf16[256,4096]{1,0:T(8,128)(2,1)S(1)} %get-tuple-element.54, f32[256,4096]{1,0:T(8,128)S(1)} %get-tuple-element.50, f32[256]{0:T(256)S(1)} %multiply_multiply_fusion, f32[256]{0:T(256)S(1)} %fusion.59), kind=kOutput, calls=%fused_computation.115 | convolution fusion | flops 207618048 | bytes 6572032 | tf_op jit(solution)/shard_map/while/body/eval_jaxpr/transpose(jvp())/dot_general | solution.py:31
  138.5 2.5 fusion.8
  142.4 1.5 collective-permute-start
  144.0 1.6 collective-permute-start.1
  146.2 2.5 collective-permute-start.3
  148.7 1.5 collective-permute-start.4
  150.3 3.4 %collective-permute-start.5 = (bf16[1,16384]{1,0:T(2,128)(2,1)S(1)}, bf16[1,16384]{1,0:T(2,128)(2,1)S(1)}, u32[]{:S(2)}, u32[]{:S(2)}) collective-permute-start(bf16[1,16384]{1,0:T(2,128)(2,1)S(1)} %dynamic_slice.38), channel_id=1, source_target_pairs={{0,24},{4,28},{8,16},{12,20},{16,8},{20,12},{24,0},{28,4},{1,25},{... | collective-permute-start | bytes 98312 | tf_op jit(solution)/shard_map/ppermute | solution.py:21
  154.2 1.1 dynamic_update_slice.30
  155.4 1.1 dynamic_update_slice.31
  156.5 1.1 dynamic_update_slice.32
  157.7 1.1 dynamic_update_slice.33
  158.8 1.1 dynamic_update_slice.34
  160.0 1.1 dynamic_update_slice.35
  161.1 1.4 dynamic_update_slice.36
  162.6 1.1 dynamic_update_slice.37
  165.1 16.2 %all-gather.8.cloned.1.call-done = bf16[32,16384]{1,0:T(8,128)(2,1)} async-done(((bf16[8,16384]{1,0:T(8,128)(2,1)}), bf16[32,16384]{1,0:T(8,128)(2,1)}) %all-gather.8.cloned.1.call-update) | async-done | bytes 1048592 | tf_op jit(solution)/shard_map/all_gather | solution.py:101
  181.3 16.1 %fusion.79 = f32[32,1024]{1,0:T(8,128)} fusion(bf16[32,16384]{1,0:T(8,128)(2,1)} %all-gather.8.cloned.1.call-done, bf16[1024,16384]{1,0:T(8,128)(2,1)} %param.13), kind=kOutput, calls=%fused_computation.120 | convolution fusion | flops 1073741824 | bytes 34734080 | tf_op jit(solution)/shard_map/dot_general | solution.py:106
  197.4 14.9 %convolution_convert_fusion = bf16[1024,16384]{1,0:T(8,128)(2,1)} fusion(bf16[32,16384]{1,0:T(8,128)(2,1)S(1)} %copy-done.6, f32[32,1024]{1,0:T(8,128)S(1)} %convolution_add_fusion), kind=kOutput, calls=%fused_computation.1 | convolution fusion | flops 1090584576 | bytes 34734080 | tf_op jit(solution)/shard_map/dot_general | solution.py:103
  212.3 55.7 %all-reduce.2.cloned.1.call-done = f32[32,1024]{1,0:T(8,128)} async-done(((f32[32,1024]{1,0:T(8,128)}), f32[32,1024]{1,0:T(8,128)}) %all-reduce.2.cloned.1.call-update) | async-done | bytes 131088 | tf_op jit(solution)/shard_map/psum | solution.py:111
  268.0 2.5 fusion.40
  (72 shorter events, 6.5 us)
Async XLA Ops:
  7.2 2.5 copy-start
  7.2 52.3 %reduce-scatter.2.cloned.1.call-start = ((), (), s32[]{:S(2)}) async-start(), calls=%async_computation.2 | async-start | bytes 2621440 | tf_op jit(solution)/shard_map/reduce_scatter | solution.py:86
  25.4 58.2 %copy-start.8 = (s32[1,256]{1,0:T(1,128)S(1)}, s32[1,256]{1,0:T(1,128)}, u32[]{:S(2)}) copy-start(s32[1,256]{1,0:T(1,128)} %param.14) | copy-start | bytes 3076
  25.4 58.2 %all-gather.4.cloned.1.call-start = ((), (), s32[]{:S(2)}) async-start(), calls=%async_computation.3 | async-start | bytes 2621440 | tf_op jit(solution)/shard_map/all_gather | solution.py:78
  26.2 81.6 %all-gather.6.cloned.1.call-start = ((), (), s32[]{:S(2)}) async-start(), calls=%async_computation.4 | async-start | bytes 2621440 | tf_op jit(solution)/shard_map/all_gather | solution.py:79
  62.8 25.2 %all-to-all-start = ((bf16[8,2,8192]{2,1,0:T(2,128)(2,1)}), bf16[8,2,8192]{2,1,0:T(2,128)(2,1)S(1)}, u32[]{:S(2)}, u32[]{:S(2)}) async-start(bf16[8,2,8192]{2,1,0:T(2,128)(2,1)} %reshape.153), calls=%async_computation.1 | async-start | bytes 524288 | tf_op jit(solution)/shard_map/all_to_all | solution.py:92
  68.3 113.0 %all-gather.8.cloned.1.call-start = ((), (), s32[]{:S(2)}) async-start(), calls=%async_computation.5 | async-start | bytes 1310720 | tf_op jit(solution)/shard_map/all_gather | solution.py:101
  91.2 5.1 %copy-start.2 = (f32[256,4096]{1,0:T(8,128)S(1)}, f32[256,4096]{1,0:T(8,128)}, u32[]{:S(2)}) copy-start(f32[256,4096]{1,0:T(8,128)} %get-tuple-element.42) | copy-start | bytes 12582916
  100.6 11.1 %copy-start.9 = (s32[1,256]{1,0:T(1,128)S(1)}, s32[1,256]{1,0:T(1,128)}, u32[]{:S(2)}) copy-start(s32[1,256]{1,0:T(1,128)} %param.15) | copy-start | bytes 3076
  107.8 4.6 %copy-start.4 = (f32[256,4096]{1,0:T(8,128)S(1)}, f32[256,4096]{1,0:T(8,128)}, u32[]{:S(2)}) copy-start(f32[256,4096]{1,0:T(8,128)} %get-tuple-element.44) | copy-start | bytes 12582916
  107.8 4.7 %copy-start.5 = (bf16[256,4096]{1,0:T(8,128)(2,1)S(1)}, bf16[256,4096]{1,0:T(8,128)(2,1)}, u32[]{:S(2)}) copy-start(bf16[256,4096]{1,0:T(8,128)(2,1)} %all-gather.6.cloned.1.call-done) | copy-start | bytes 6291460
  116.3 3.1 %copy-start.3 = (f32[256,4096]{1,0:T(8,128)S(1)}, f32[256,4096]{1,0:T(8,128)}, u32[]{:S(2)}) copy-start(f32[256,4096]{1,0:T(8,128)} %get-tuple-element.42) | copy-start | bytes 12582916
  142.4 7.9 %collective-permute-start = (bf16[1,16384]{1,0:T(2,128)(2,1)S(1)}, bf16[1,16384]{1,0:T(2,128)(2,1)S(1)}, u32[]{:S(2)}, u32[]{:S(2)}) collective-permute-start(bf16[1,16384]{1,0:T(2,128)(2,1)S(1)} %dynamic_slice.33), channel_id=1, source_target_pairs={{0,4},{4,0},{8,12},{12,8},{16,20},{20,16},{24,28},{28,24},{1,5},{5... | collective-permute-start | bytes 98312 | tf_op jit(solution)/shard_map/ppermute | solution.py:21
  144.0 9.7 %collective-permute-start.1 = (bf16[1,16384]{1,0:T(2,128)(2,1)S(1)}, bf16[1,16384]{1,0:T(2,128)(2,1)S(1)}, u32[]{:S(2)}, u32[]{:S(2)}) collective-permute-start(bf16[1,16384]{1,0:T(2,128)(2,1)S(1)} %dynamic_slice.34), channel_id=1, source_target_pairs={{0,8},{4,12},{8,0},{12,4},{16,24},{20,28},{24,16},{28,20},{1,9},{5... | collective-permute-start | bytes 98312 | tf_op jit(solution)/shard_map/ppermute | solution.py:21
  145.5 12.1 %collective-permute-start.2 = (bf16[1,16384]{1,0:T(2,128)(2,1)S(1)}, bf16[1,16384]{1,0:T(2,128)(2,1)S(1)}, u32[]{:S(2)}, u32[]{:S(2)}) collective-permute-start(bf16[1,16384]{1,0:T(2,128)(2,1)S(1)} %dynamic_slice.35), channel_id=1, source_target_pairs={{0,12},{4,8},{8,4},{12,0},{16,28},{20,24},{24,20},{28,16},{1,13},{... | collective-permute-start | bytes 98312 | tf_op jit(solution)/shard_map/ppermute | solution.py:21
  146.2 12.6 %collective-permute-start.3 = (bf16[1,16384]{1,0:T(2,128)(2,1)S(1)}, bf16[1,16384]{1,0:T(2,128)(2,1)S(1)}, u32[]{:S(2)}, u32[]{:S(2)}) collective-permute-start(bf16[1,16384]{1,0:T(2,128)(2,1)S(1)} %dynamic_slice.36), channel_id=1, source_target_pairs={{0,16},{4,20},{8,24},{12,28},{16,0},{20,4},{24,8},{28,12},{1,17},{... | collective-permute-start | bytes 98312 | tf_op jit(solution)/shard_map/ppermute | solution.py:21
  148.7 11.3 %collective-permute-start.4 = (bf16[1,16384]{1,0:T(2,128)(2,1)S(1)}, bf16[1,16384]{1,0:T(2,128)(2,1)S(1)}, u32[]{:S(2)}, u32[]{:S(2)}) collective-permute-start(bf16[1,16384]{1,0:T(2,128)(2,1)S(1)} %dynamic_slice.37), channel_id=1, source_target_pairs={{0,20},{4,16},{8,28},{12,24},{16,4},{20,0},{24,12},{28,8},{1,21},{... | collective-permute-start | bytes 98312 | tf_op jit(solution)/shard_map/ppermute | solution.py:21
  150.3 10.9 %collective-permute-start.5 = (bf16[1,16384]{1,0:T(2,128)(2,1)S(1)}, bf16[1,16384]{1,0:T(2,128)(2,1)S(1)}, u32[]{:S(2)}, u32[]{:S(2)}) collective-permute-start(bf16[1,16384]{1,0:T(2,128)(2,1)S(1)} %dynamic_slice.38), channel_id=1, source_target_pairs={{0,24},{4,28},{8,16},{12,20},{16,8},{20,12},{24,0},{28,4},{1,25},{... | collective-permute-start | bytes 98312 | tf_op jit(solution)/shard_map/ppermute | solution.py:21
  153.7 8.9 %collective-permute-start.6 = (bf16[1,16384]{1,0:T(2,128)(2,1)S(1)}, bf16[1,16384]{1,0:T(2,128)(2,1)S(1)}, u32[]{:S(2)}, u32[]{:S(2)}) collective-permute-start(bf16[1,16384]{1,0:T(2,128)(2,1)S(1)} %dynamic_slice.39), channel_id=1, source_target_pairs={{0,28},{4,24},{8,20},{12,16},{16,12},{20,8},{24,4},{28,0},{1,29},{... | collective-permute-start | bytes 98312 | tf_op jit(solution)/shard_map/ppermute | solution.py:21
  163.7 0.7 copy-start.7
  164.4 103.6 %all-reduce.2.cloned.1.call-start = ((), (), s32[]{:S(2)}) async-start(), calls=%async_computation.6 | async-start | bytes 262144 | tf_op jit(solution)/shard_map/psum | solution.py:111
  181.3 16.1 %copy-start.6 = (bf16[32,16384]{1,0:T(8,128)(2,1)S(1)}, bf16[32,16384]{1,0:T(8,128)(2,1)}, u32[]{:S(2)}) copy-start(bf16[32,16384]{1,0:T(8,128)(2,1)} %all-gather.8.cloned.1.call-done) | copy-start | bytes 3145732
  197.4 73.1 %copy-start.1 = (bf16[256,1024]{1,0:T(8,128)(2,1)S(1)}, bf16[256,1024]{1,0:T(8,128)(2,1)}, u32[]{:S(2)}) copy-start(bf16[256,1024]{1,0:T(8,128)(2,1)} %param.11) | copy-start | bytes 1572868
Sparse Core Ops, SparseCore 0:
  25.6 33.9 reduce-scatter.1
  61.1 22.5 all-gather.3
  85.2 22.5 all-gather.5
  164.5 16.6 all-gather.7
  197.5 70.4 all-reduce.1
